TPU v7x, 32 devices: a whole 2x2x4 slice. The times are simulated.
32 devices in a mesh: dp: 2 (over core), seq: 16 (over z, y, x).
Axes of the slice: x: 2, y: 2, z: 4, core: 2. Of those that a mesh axis runs over, the one named last changes fastest.
Arguments:
- latent: bfloat16 [32, 1024, 1152], P(('dp', 'seq')), parts along dimension 0, may hold values from -6 to 6
- w_qkv_space: bfloat16 [1152, 1728], replicated, may hold values from -0.1875 to 0.1875
- w_out_space: bfloat16 [576, 1152], replicated, may hold values from -0.25 to 0.25
- w_qkv_time: bfloat16 [1152, 1728], replicated, may hold values from -0.1875 to 0.1875
- w_out_time: bfloat16 [576, 1152], replicated, may hold values from -0.25 to 0.25
- modulation: float32 [12, 1152], P('dp'), parts along dimension 0, may hold values from -1.5 to 5
Outputs:
- block_out: bfloat16 [32, 1024, 1152], P(('dp', 'seq')), parts along dimension 0
There are 2 independent parts, one for each index of `dp`. A program takes and returns all parts, laid end to end along the dimension named above; an argument that names none is the same for every part. Nothing has to cross between parts.
All inputs are finite; a program needn't handle non-finite values.
Results may differ from a plain program's by a relative error of at most 0.02.
The roundings to bfloat16 on the way count: a program that leaves them out, or rounds other values in their place, can miss the bound.
Values may be sent and summed in bfloat16 or wider, within the bound.
No kernel may reach another device: no remote copies, remote signals or barrier semaphores. Data moves between devices by JAX's collectives and lax.ppermute only.
A program may use at most 128 MiB of HBM per device.

v0:
```python
import jax
import jax.numpy as jnp
from jax import lax
from jax.sharding import PartitionSpec as P

HEADS = 8
HEAD_DIM = 72
EPS = 1e-06


def normalize(values):
    center = jnp.mean(values, -1, keepdims=True)
    centred = values - center
    spread = jnp.mean(centred * centred, -1, keepdims=True)
    return centred * lax.rsqrt(spread + EPS)


def modulated(latent, modulation, first):
    normed = normalize(latent.astype(jnp.float32))
    return (normed * (1.0 + modulation[first + 1]) + modulation[first]).astype(jnp.bfloat16)


def softmax_weights(scores, axis):
    top_score = jnp.max(scores, axis, keepdims=True)
    expo = jnp.exp(scores - top_score)
    return (expo / jnp.sum(expo, axis, keepdims=True)).astype(jnp.bfloat16)


def attend_space(frame_rows, w_qkv, w_out, modulation):
    tokens_here = frame_rows.shape[0]
    mixed = modulated(frame_rows, modulation, 0)
    triple = jnp.dot(mixed, w_qkv, preferred_element_type=jnp.float32).astype(jnp.bfloat16)
    triple = triple.reshape(tokens_here, 3, HEADS, HEAD_DIM)
    factor = 1.0 / float(HEAD_DIM) ** 0.5
    scores = (
        jnp.einsum("shd,thd->hst", triple[:, 0], triple[:, 1], preferred_element_type=jnp.float32)
        * factor
    )
    weights = softmax_weights(scores, 2)
    outputs = jnp.einsum(
        "hst,thd->shd", weights, triple[:, 2], preferred_element_type=jnp.float32
    ).astype(jnp.bfloat16)
    delta = jnp.dot(
        outputs.reshape(tokens_here, HEADS * HEAD_DIM), w_out, preferred_element_type=jnp.float32
    )
    return (frame_rows.astype(jnp.float32) + modulation[2] * delta).astype(jnp.bfloat16)


def attend_time(queries, key_heads, value_heads):
    factor = 1.0 / float(queries.shape[-1]) ** 0.5
    scores = (
        jnp.einsum("fphd,gphd->phfg", queries, key_heads, preferred_element_type=jnp.float32)
        * factor
    )
    weights = softmax_weights(scores, 3)
    return jnp.einsum(
        "phfg,gphd->fphd", weights, value_heads, preferred_element_type=jnp.float32
    ).astype(jnp.bfloat16)


def shards(latent, w_qkv_space, w_out_space, w_qkv_time, w_out_time, modulation):
    after_space = attend_space(latent[0], w_qkv_space, w_out_space, modulation)
    spatial, width = after_space.shape
    patches = lax.all_to_all(after_space[None], "seq", split_axis=1, concat_axis=0, tiled=True)
    frames, positions, width = patches.shape
    mixed = modulated(patches, modulation, 3).reshape(frames * positions, width)
    triple = jnp.dot(mixed, w_qkv_time, preferred_element_type=jnp.float32).astype(jnp.bfloat16)
    triple = triple.reshape(frames, positions, 3, HEADS, HEAD_DIM)
    outputs = attend_time(triple[:, :, 0], triple[:, :, 1], triple[:, :, 2])
    delta = jnp.dot(
        outputs.reshape(frames * positions, HEADS * HEAD_DIM),
        w_out_time,
        preferred_element_type=jnp.float32,
    )
    result = patches.astype(jnp.float32).reshape(frames * positions, width) + modulation[5] * delta
    result = result.astype(jnp.bfloat16).reshape(frames, positions, width)
    return lax.all_to_all(result, "seq", split_axis=0, concat_axis=1, tiled=True)


def solution(mesh):
    in_specs = (P(("dp", "seq"), None, None), P(), P(), P(), P(), P("dp", None))
    out_specs = P(("dp", "seq"), None, None)
    return jax.shard_map(shards, mesh=mesh, in_specs=in_specs, out_specs=out_specs, check_vma=False)
```

profile of v0, /device:TPU:0, one launch (start us, length us, event | category | flops | bytes accessed | tf_op | source)
XLA Modules:
  0.0 269.0 jit_solution(783976993422969830)
XLA Ops:
  0.0 0.0 copy-start
  0.0 0.0 copy-start.2
  0.0 1.2 slice_reduce_fusion.1
  1.2 2.1 convert_reduce_fusion.1
  3.3 0.0 copy-done.2
  3.3 0.8 fusion.13
  4.0 9.2 %convolution_convert_fusion.1 = bf16[1024,1728]{0,1:T(8,128)(2,1)} fusion(bf16[1152,1728]{0,1:T(8,128)(2,1)} %param.7, bf16[1,1024,1152]{2,1,0:T(8,128)(2,1)S(1)} %copy-done.2, f32[1152]{0:T(1024)S(1)} %get-tuple-element.6, f32[1152]{0:T(1024)S(1)} %get-tuple-element.7, f32[1024]{0:T(1024)S(1)} %add_rsqrt_fusion.1, f32[1024]{0:T(1024)S(1)} %broadcast_multiply_fusion.1), kind=kOutput, calls=%fused_computation.36 | convolution fusion | flops 4085710848 | bytes 9896960 | tf_op jit(solution)/shard_map/dot_general | solution.py:32
  13.2 17.8 %fusion.55 = (f32[8,1024]{1,0:T(8,128)S(1)}, f32[8,1024,1024]{1,2,0:T(8,128)}) fusion(bf16[1024,3,8,72]{0,3,2,1:T(8,128)(2,1)} %bitcast.104), kind=kOutput, calls=%fused_computation.75 | convolution fusion | flops 1233126400 | bytes 35946496 | tf_op jit(solution)/shard_map/sub | solution.py:25
  31.0 0.0 copy-start.3
  31.1 12.8 %fusion.50 = bf16[8,72,1024]{2,1,0:T(8,128)(2,1)S(1)} fusion(f32[8,1024,1024]{1,2,0:T(8,128)} %get-tuple-element.17, f32[8,1024]{1,0:T(8,128)S(1)} %get-tuple-element.16, bf16[1024,3,8,72]{0,3,2,1:T(8,128)(2,1)} %bitcast.105), kind=kOutput, calls=%fused_computation.57 | convolution fusion | flops 1225326592 | bytes 35946496 | tf_op jit(solution)/shard_map/hst,thd->shd/dot_general | solution.py:40
  43.9 0.0 copy-done
  43.9 0.0 copy-done.3
  43.9 2.4 fusion.26
  46.3 5.8 %copy.37 = bf16[1,1024,1152]{2,0,1:T(2,128)(2,1)} copy(bf16[1,1024,1152]{2,1,0:T(8,128)(2,1)S(1)} %fusion.26) | data formatting | bytes 4718592 | tf_op jit(solution)/shard_map/broadcast_in_dim | solution.py:64
  52.1 0.5 broadcast.73
  52.6 16.3 %reduce.15 = bf16[1024,1152]{1,0:T(8,128)(2,1)} reduce(bf16[1024,1,1152]{2,1,0:T(2,128)(2,1)} %bitcast.100, bf16[]{:T(256)} %broadcast.73), dimensions={1}, to_apply=%bitcast.99.reduce_sub_computation | reduce | bytes 4718594
  68.9 4.1 %reshape.90 = bf16[16,2,36864]{2,1,0:T(2,128)(2,1)} reshape(bf16[1024,1152]{1,0:T(8,128)(2,1)} %reduce.15) | data formatting | bytes 4718592
  73.0 63.4 %all_to_all.21 = bf16[16,2,36864]{2,1,0:T(2,128)(2,1)} all-to-all(bf16[16,2,36864]{2,1,0:T(2,128)(2,1)} %reshape.90), channel_id=1, replica_groups=mesh['dp'=2,'seq'=16] {'seq'}, dimensions={0} | all-to-all | bytes 4718592 | tf_op jit(solution)/shard_map/all_to_all | solution.py:64
  136.4 10.7 %reshape.91 = bf16[1024,1,1152]{2,1,0:T(2,128)(2,1)} reshape(bf16[16,2,36864]{2,1,0:T(2,128)(2,1)} %all_to_all.21) | data formatting | bytes 4718592
  147.1 0.0 copy-start.4
  147.1 2.9 %convert_reduce_fusion = (f32[1024]{0:T(1024)S(1)}, bf16[1,1024,1152]{2,1,0:T(8,128)(2,1)S(1)}) fusion(bf16[1,1024,1152]{2,0,1:T(2,128)(2,1)} %bitcast.101), kind=kLoop, calls=%fused_computation.9 | loop fusion | flops 2358272 | bytes 4722688 | tf_op jit(solution)/shard_map/reduce_sum | solution.py:12
  150.0 0.0 copy-start.1
  150.1 0.8 fusion.24
  150.8 0.6 copy-done.1
  151.5 0.0 copy-done.4
  151.5 7.1 %convolution_convert_fusion = bf16[1024,1728]{0,1:T(8,128)(2,1)} fusion(bf16[1152,1728]{0,1:T(8,128)(2,1)S(1)} %copy-done.4, bf16[1,1024,1152]{2,1,0:T(8,128)(2,1)S(1)} %get-tuple-element.12, f32[1152]{0:T(1024)S(1)} %get-tuple-element.9, f32[1152]{0:T(1024)S(1)} %get-tuple-element.10, f32[1024]{0:T(1024)S(1)} %add_rsqrt_fusion, ...), kind=kOutput, calls=%fused_computation.35 | convolution fusion | flops 4085710848 | bytes 9896960 | tf_op jit(solution)/shard_map/dot_general | solution.py:67
  158.6 9.9 %reshape.83 = bf16[16,64,3,8,72]{1,0,4,3,2:T(8,128)(2,1)} reshape(bf16[1024,1728]{0,1:T(8,128)(2,1)} %convolution_convert_fusion) | data formatting | bytes 7077888 | tf_op jit(solution)/shard_map/reshape | solution.py:68
  168.5 6.7 %fusion.54 = (bf16[16,64,1,8,72]{1,0,4,3,2:T(8,128)(2,1)}, bf16[16,64,1,8,72]{1,0,4,3,2:T(8,128)(2,1)}, bf16[16,64,1,8,72]{1,0,4,3,2:T(8,128)(2,1)}) fusion(bf16[16,64,3,8,72]{1,0,4,3,2:T(8,128)(2,1)} %reshape.83), kind=kLoop, calls=%fused_computation.74 | loop fusion | bytes 7077888 | tf_op jit(solution)/shard_map/slice | solution.py:69
  175.3 5.4 %copy.33 = bf16[16,64,1,8,72]{4,0,3,1,2:T(8,128)(2,1)S(1)} copy(bf16[16,64,1,8,72]{1,0,4,3,2:T(8,128)(2,1)} %get-tuple-element.14) | data formatting | bytes 2359296
  180.6 6.3 %copy.34 = bf16[16,64,1,8,72]{4,0,3,1,2:T(8,128)(2,1)} copy(bf16[16,64,1,8,72]{1,0,4,3,2:T(8,128)(2,1)} %get-tuple-element.15) | data formatting | bytes 2359296
  186.9 2.8 %fusion.42 = f32[64,8,16,16]{2,3,1,0:T(8,128)S(1)} fusion(bf16[16,64,1,8,72]{4,0,3,1,2:T(8,128)(2,1)} %copy.34, bf16[16,64,1,8,72]{4,0,3,1,2:T(8,128)(2,1)S(1)} %copy.33), kind=kOutput, calls=%fused_computation.50 | convolution fusion | flops 18874368 | bytes 2883584 | tf_op jit(solution)/shard_map/fphd,gphd->phfg/dot_general | solution.py:52
  189.7 4.2 %fusion.56 = (f32[64,8,16]{2,1,0:T(8,128)}, f32[64,8,16,16]{2,3,1,0:T(8,128)}) fusion(f32[64,8,16,16]{2,3,1,0:T(8,128)S(1)} %fusion.42), kind=kOutput, calls=%fused_computation.76 | output fusion | flops 524303 | bytes 1081344 | tf_op jit(solution)/shard_map/sub | solution.py:25
  193.9 5.4 %copy.32 = bf16[16,64,1,8,72]{4,0,3,1,2:T(8,128)(2,1)S(1)} copy(bf16[16,64,1,8,72]{1,0,4,3,2:T(8,128)(2,1)} %get-tuple-element.13) | data formatting | bytes 2359296
  199.3 3.1 %convert_bitcast_fusion.2 = bf16[16,64,8,72]{3,0,2,1:T(8,128)(2,1)S(1)} fusion(f32[64,8,16,16]{2,3,1,0:T(8,128)} %get-tuple-element.19, f32[64,8,16]{2,1,0:T(8,128)} %get-tuple-element.18, bf16[16,64,1,8,72]{4,0,3,1,2:T(8,128)(2,1)S(1)} %copy.32), kind=kOutput, calls=%fused_computation.54 | convolution fusion | flops 19726336 | bytes 2916352 | tf_op jit(solution)/shard_map/phfg,gphd->fphd/dot_general | solution.py:56
  202.3 0.5 copy.27
  202.9 2.5 reshape.80
  205.4 4.6 %fusion.22 = bf16[1024,1152]{1,0:T(8,128)(2,1)S(1)} fusion(bf16[1,1024,1152]{2,1,0:T(8,128)(2,1)} %copy-done.1, bf16[1024,576]{1,0:T(8,128)(2,1)} %reshape.80, bf16[576,1152]{1,0:T(8,128)(2,1)} %param.10, f32[1152]{0:T(1024)S(1)} %get-tuple-element.5), kind=kOutput, calls=%fused_computation.30 | convolution fusion | flops 1363673088 | bytes 7229952 | tf_op jit(solution)/shard_map/dot_general | solution.py:70
  210.0 57.6 %all_to_all.22 = bf16[16,64,1152]{2,1,0:T(8,128)(2,1)S(1)} all-to-all(bf16[16,64,1152]{2,1,0:T(8,128)(2,1)S(1)} %bitcast.103), channel_id=1, replica_groups=mesh['dp'=2,'seq'=16] {'seq'}, dimensions={0} | all-to-all | bytes 4718592 | tf_op jit(solution)/shard_map/all_to_all | solution.py:77
  267.6 1.4 copy.39
  (4 shorter events, 0.0 us)
Async XLA Ops:
  0.0 43.9 %copy-start = (bf16[576,1152]{1,0:T(8,128)(2,1)S(1)}, bf16[576,1152]{1,0:T(8,128)(2,1)}, u32[]{:S(2)}) copy-start(bf16[576,1152]{1,0:T(8,128)(2,1)} %param.8) | copy-start | bytes 3981316
  0.0 3.3 %copy-start.2 = (bf16[1,1024,1152]{2,1,0:T(8,128)(2,1)S(1)}, bf16[1,1024,1152]{2,1,0:T(8,128)(2,1)}, u32[]{:S(2)}) copy-start(bf16[1,1024,1152]{2,1,0:T(8,128)(2,1)} %param.6) | copy-start | bytes 7077892
  31.0 12.9 %copy-start.3 = (bf16[1,1024,1152]{2,1,0:T(8,128)(2,1)S(1)}, bf16[1,1024,1152]{2,1,0:T(8,128)(2,1)}, u32[]{:S(2)}) copy-start(bf16[1,1024,1152]{2,1,0:T(8,128)(2,1)} %param.6) | copy-start | bytes 7077892
  147.1 4.3 %copy-start.4 = (bf16[1152,1728]{0,1:T(8,128)(2,1)S(1)}, bf16[1152,1728]{0,1:T(8,128)(2,1)}, u32[]{:S(2)}) copy-start(bf16[1152,1728]{0,1:T(8,128)(2,1)} %param.9) | copy-start | bytes 11943940
  150.0 1.4 copy-start.1
where the time goes:
time: 270 us; the launch traced here: 269 us
  blocking collectives  121 us (45%)
  local copies, waits for them, and re-layouts  59.8 us (22%)
  matrix products  59.8 us (22%)
  other arithmetic  28.2 us (10%)
    all_to_all x1, blocking collectives, shards(): lax.all_to_all(after_space[None], 'seq', split_axis=1, concat_axis=0, til...  63.4 us
    all_to_all x1, blocking collectives, shards(): lax.all_to_all(result, 'seq', split_axis=0, concat_axis=1, tiled=True)  57.6 us
    unnamed x17, local copies, waits for them, and re-layouts  34.3 us
    sub x1, matrix products, softmax_weights(): expo = jnp.exp(scores - top_score)  17.8 us
    unnamed x1, other arithmetic  16.3 us
    dot_general x1, matrix products, attend_space(): jnp.einsum('hst,thd->shd', weights, triple[:, 2], preferred_element_type=...  12.8 us
    reshape x1, local copies, waits for them, and re-layouts, shards(): triple = triple.reshape(frames, positions, 3, HEADS, HEAD_DIM)  9.93 us
    dot_general x1, matrix products, attend_space(): jnp.dot(mixed, w_qkv, preferred_element_type=jnp.float32)  9.17 us

commit v1 on v0

--- a/solution.py
+++ b/solution.py
@@ -1,11 +1,21 @@
+import functools
 import jax
 import jax.numpy as jnp
 from jax import lax
 from jax.sharding import PartitionSpec as P
+from jax.lax import all_to_all, axis_size
 
 HEADS = 8
 HEAD_DIM = 72
 EPS = 1e-06
+
+
+def order_units_now(panel, link_axis):
+    y = jnp.stack(jnp.split(panel, axis_size(link_axis), 1), 0)
+    return jnp.concatenate(all_to_all(y, link_axis, 0, 0), 0)
+
+
+enter_ends = functools.partial(order_units_now, link_axis="seq")
 
 
 def normalize(values):
@@ -61,7 +71,7 @@
 def shards(latent, w_qkv_space, w_out_space, w_qkv_time, w_out_time, modulation):
     after_space = attend_space(latent[0], w_qkv_space, w_out_space, modulation)
     spatial, width = after_space.shape
-    patches = lax.all_to_all(after_space[None], "seq", split_axis=1, concat_axis=0, tiled=True)
+    patches = enter_ends(after_space[None])
     frames, positions, width = patches.shape
     mixed = modulated(patches, modulation, 3).reshape(frames * positions, width)
     triple = jnp.dot(mixed, w_qkv_time, preferred_element_type=jnp.float32).astype(jnp.bfloat16)

time: 270 us -> 244 us (0.904)
  local copies, waits for them, and re-layouts: 59.8 us -> 41.3 us
  other arithmetic: 28.2 us -> 24.7 us
  matrix products: 59.8 us -> 56.7 us
    unnamed x1 -> x0, other arithmetic: 16.3 us -> none
    unnamed x17 -> x33, local copies, waits for them, and re-layouts: 34.3 us -> 21.4 us
    sub x1, other arithmetic: 4.17 us -> 16.1 us  [softmax_weights(): expo = jnp.exp(scores - top_score)]
    broadcast_in_dim x1 -> x0, local copies, waits for them, and re-layouts: 5.76 us -> none  [shards(): after_space[None]]
    convert_element_type x0 -> x1, other arithmetic: none -> 2.75 us  [modulated(): (normed * (1.0 + modulation[first + 1]) + modulation[first]).astype(jnp.b...]
where the time goes in v1:
time: 244 us
  blocking collectives  121 us (50%)
  matrix products  56.7 us (23%)
  local copies, waits for them, and re-layouts  41.3 us (17%)
  other arithmetic  24.7 us (10%)
    all_to_all x1, blocking collectives, order_units_now(): return jnp.concatenate(all_to_all(y, link_axis, 0, 0), 0)  63.1 us
    all_to_all x1, blocking collectives, shards(): lax.all_to_all(result, 'seq', split_axis=0, concat_axis=1, tiled=True)  57.6 us
    unnamed x33, local copies, waits for them, and re-layouts  21.4 us
    sub x1, matrix products, softmax_weights(): expo = jnp.exp(scores - top_score)  17.8 us
    sub x1, other arithmetic, softmax_weights(): expo = jnp.exp(scores - top_score)  16.1 us
    dot_general x1, matrix products, attend_space(): jnp.einsum('hst,thd->shd', weights, triple[:, 2], preferred_element_type=...  12.7 us
    reshape x1, local copies, waits for them, and re-layouts, shards(): triple = triple.reshape(frames, positions, 3, HEADS, HEAD_DIM)  9.93 us
    dot_general x1, matrix products, attend_space(): jnp.dot(mixed, w_qkv, preferred_element_type=jnp.float32)  9.16 us

profile of v1, /device:TPU:0, one launch (start us, length us, event | category | flops | bytes accessed | tf_op | source)
XLA Modules:
  0.0 243.7 jit_solution(10484469426005071835)
XLA Ops:
  0.0 0.0 copy-start
  0.0 0.0 copy-start.2
  0.0 0.0 copy-start.5
  0.0 2.2 convert_reduce_fusion
  2.2 0.3 copy-done.2
  2.5 0.8 fusion.11
  3.3 0.0 copy-done.5
  3.3 0.1 slice_reduce_fusion.1
  3.4 9.2 %convolution_convert_fusion.1 = bf16[1024,1728]{0,1:T(8,128)(2,1)} fusion(bf16[1152,1728]{0,1:T(8,128)(2,1)} %param.7, bf16[1,1024,1152]{2,1,0:T(8,128)(2,1)S(1)} %copy-done.2, f32[1152]{0:T(1024)S(1)} %get-tuple-element.6, f32[1152]{0:T(1024)S(1)} %get-tuple-element.7, f32[1024]{0:T(1024)S(1)} %add_rsqrt_fusion.1, f32[1024]{0:T(1024)S(1)} %broadcast_multiply_fusion.1), kind=kOutput, calls=%fused_computation.35 | convolution fusion | flops 4085710848 | bytes 9896960 | tf_op jit(solution)/shard_map/dot_general | solution.py:42
  12.5 17.8 %fusion.64 = (f32[8,1024]{1,0:T(8,128)S(1)}, f32[8,1024,1024]{1,2,0:T(8,128)}) fusion(bf16[1024,3,8,72]{0,3,2,1:T(8,128)(2,1)} %bitcast.165), kind=kOutput, calls=%fused_computation.102 | convolution fusion | flops 1233126400 | bytes 35946496 | tf_op jit(solution)/shard_map/sub | solution.py:35
  30.4 0.0 copy-start.3
  30.4 12.7 %fusion.43 = bf16[8,72,1024]{2,1,0:T(8,128)(2,1)S(1)} fusion(f32[8,1024,1024]{1,2,0:T(8,128)} %get-tuple-element.15, f32[8,1024]{1,0:T(8,128)S(1)} %get-tuple-element.14, bf16[1024,3,8,72]{0,3,2,1:T(8,128)(2,1)} %bitcast.166), kind=kOutput, calls=%fused_computation.52 | convolution fusion | flops 1225326592 | bytes 35946496 | tf_op jit(solution)/shard_map/hst,thd->shd/dot_general | solution.py:50
  43.0 0.0 copy-done
  43.0 0.0 copy-done.3
  43.0 2.4 fusion.24
  45.8 63.1 %all_to_all.17 = bf16[16,1,64,1152]{3,2,1,0:T(8,128)(2,1)S(1)} all-to-all(bf16[16,1,64,1152]{3,2,1,0:T(8,128)(2,1)S(1)} %fusion.45), channel_id=1, replica_groups=mesh['dp'=2,'seq'=16] {'seq'}, dimensions={0} | all-to-all | bytes 4718592 | tf_op jit(solution)/shard_map/all_to_all | solution.py:15
  108.9 0.0 copy-start.1
  108.9 1.4 copy-done.1
  110.3 0.4 convert_reduce_fusion.1
  110.7 0.1 div.35
  110.8 2.4 fusion.17
  113.2 0.1 rsqrt.21
  113.3 0.0 copy-start.6
  113.3 2.7 %fusion.21 = bf16[1024,1152]{1,0:T(8,128)(2,1)S(1)} fusion(bf16[16,1,64,1152]{3,2,1,0:T(8,128)(2,1)} %copy-done.1, f32[1152]{0:T(1024)S(1)} %get-tuple-element.9, f32[1152]{0:T(1024)S(1)} %get-tuple-element.10, f32[1024]{0:T(1024)S(1)} %rsqrt.21, f32[1024]{0:T(1024)S(1)} %div.35), kind=kLoop, calls=%fused_computation.30 | loop fusion | flops 7077888 | bytes 4736000 | tf_op jit(solution)/shard_map/convert_element_type | solution.py:30
  116.1 0.1 copy-done.6
  116.2 6.2 %convolution_convert_fusion = bf16[1024,1728]{0,1:T(8,128)(2,1)} fusion(bf16[1024,1152]{1,0:T(8,128)(2,1)S(1)} %fusion.21, bf16[1152,1728]{0,1:T(8,128)(2,1)S(1)} %copy-done.6), kind=kOutput, calls=%fused_computation.34 | convolution fusion | flops 4078632960 | bytes 9879552 | tf_op jit(solution)/shard_map/dot_general | solution.py:77
  122.4 9.9 %reshape.82 = bf16[16,64,3,8,72]{1,0,4,3,2:T(8,128)(2,1)} reshape(bf16[1024,1728]{0,1:T(8,128)(2,1)} %convolution_convert_fusion) | data formatting | bytes 7077888 | tf_op jit(solution)/shard_map/reshape | solution.py:78
  132.3 6.7 %fusion.63 = (bf16[16,64,1,8,72]{1,0,4,3,2:T(8,128)(2,1)}, bf16[16,64,1,8,72]{1,0,4,3,2:T(8,128)(2,1)}, bf16[16,64,1,8,72]{1,0,4,3,2:T(8,128)(2,1)}) fusion(bf16[16,64,3,8,72]{1,0,4,3,2:T(8,128)(2,1)} %reshape.82), kind=kLoop, calls=%fused_computation.101 | loop fusion | bytes 7077888 | tf_op jit(solution)/shard_map/slice | solution.py:79
  139.0 6.3 %copy.23 = bf16[16,64,1,8,72]{4,0,3,1,2:T(8,128)(2,1)} copy(bf16[16,64,1,8,72]{1,0,4,3,2:T(8,128)(2,1)} %get-tuple-element.11) | data formatting | bytes 2359296
  145.3 5.4 %copy.24 = bf16[16,64,1,8,72]{4,0,3,1,2:T(8,128)(2,1)S(1)} copy(bf16[16,64,1,8,72]{1,0,4,3,2:T(8,128)(2,1)} %get-tuple-element.12) | data formatting | bytes 2359296
  150.7 6.3 %copy.25 = bf16[16,64,1,8,72]{4,0,3,1,2:T(8,128)(2,1)} copy(bf16[16,64,1,8,72]{1,0,4,3,2:T(8,128)(2,1)} %get-tuple-element.13) | data formatting | bytes 2359296
  156.9 2.8 %fusion.35 = f32[64,8,16,16]{2,3,1,0:T(8,128)S(1)} fusion(bf16[16,64,1,8,72]{4,0,3,1,2:T(8,128)(2,1)} %copy.25, bf16[16,64,1,8,72]{4,0,3,1,2:T(8,128)(2,1)S(1)} %copy.24), kind=kOutput, calls=%fused_computation.45 | convolution fusion | flops 18874368 | bytes 2883584 | tf_op jit(solution)/shard_map/fphd,gphd->phfg/dot_general | solution.py:62
  159.8 0.0 copy-start.4
  159.8 16.1 %fusion.65 = (f32[64,8,16]{2,1,0:T(8,128)S(1)}, f32[64,8,16,16]{2,3,1,0:T(8,128)S(1)}) fusion(f32[64,8,16,16]{2,3,1,0:T(8,128)S(1)} %fusion.35), kind=kOutput, calls=%fused_computation.103 | output fusion | flops 524303 | bytes 1081344 | tf_op jit(solution)/shard_map/sub | solution.py:35
  175.8 0.0 copy-done.4
  175.8 1.1 convert_bitcast_fusion.1
  176.9 0.5 copy.18
  177.5 2.5 %reshape.79 = bf16[1024,576]{1,0:T(8,128)(2,1)} reshape(bf16[16,64,8,72]{3,2,1,0:T(8,128)(2,1)S(1)} %copy.18) | data formatting | bytes 2359296 | tf_op jit(solution)/shard_map/reshape | solution.py:81
  180.0 4.6 %fusion.22 = bf16[1024,1152]{1,0:T(8,128)(2,1)S(1)} fusion(bf16[16,1,64,1152]{3,2,1,0:T(8,128)(2,1)} %copy-done.1, bf16[1024,576]{1,0:T(8,128)(2,1)} %reshape.79, bf16[576,1152]{1,0:T(8,128)(2,1)} %param.10, f32[1152]{0:T(1024)S(1)} %get-tuple-element.5), kind=kOutput, calls=%fused_computation.31 | convolution fusion | flops 1363673088 | bytes 7229952 | tf_op jit(solution)/shard_map/dot_general | solution.py:80
  184.6 57.6 %all_to_all.18 = bf16[16,64,1152]{2,1,0:T(8,128)(2,1)S(1)} all-to-all(bf16[16,64,1152]{2,1,0:T(8,128)(2,1)S(1)} %bitcast.164), channel_id=1, replica_groups=mesh['dp'=2,'seq'=16] {'seq'}, dimensions={0} | all-to-all | bytes 4718592 | tf_op jit(solution)/shard_map/all_to_all | solution.py:87
  242.2 1.4 copy.42
  (20 shorter events, 0.3 us)
Async XLA Ops:
  0.0 43.0 %copy-start = (bf16[576,1152]{1,0:T(8,128)(2,1)S(1)}, bf16[576,1152]{1,0:T(8,128)(2,1)}, u32[]{:S(2)}) copy-start(bf16[576,1152]{1,0:T(8,128)(2,1)} %param.8) | copy-start | bytes 3981316
  0.0 2.5 %copy-start.2 = (bf16[1,1024,1152]{2,1,0:T(8,128)(2,1)S(1)}, bf16[1,1024,1152]{2,1,0:T(8,128)(2,1)}, u32[]{:S(2)}) copy-start(bf16[1,1024,1152]{2,1,0:T(8,128)(2,1)} %param.6) | copy-start | bytes 7077892
  0.0 3.3 %copy-start.5 = (f32[6,1152]{1,0:T(8,128)S(1)}, f32[6,1152]{1,0:T(8,128)}, u32[]{:S(2)}) copy-start(f32[6,1152]{1,0:T(8,128)} %param.11) | copy-start | bytes 82948
  30.4 12.7 %copy-start.3 = (bf16[1,1024,1152]{2,1,0:T(8,128)(2,1)S(1)}, bf16[1,1024,1152]{2,1,0:T(8,128)(2,1)}, u32[]{:S(2)}) copy-start(bf16[1,1024,1152]{2,1,0:T(8,128)(2,1)} %param.6) | copy-start | bytes 7077892
  108.9 1.4 copy-start.1
  113.3 2.8 %copy-start.6 = (bf16[1152,1728]{0,1:T(8,128)(2,1)S(1)}, bf16[1152,1728]{0,1:T(8,128)(2,1)}, u32[]{:S(2)}) copy-start(bf16[1152,1728]{0,1:T(8,128)(2,1)} %param.9) | copy-start | bytes 11943940
  159.8 16.1 %copy-start.4 = (bf16[16,64,1,8,72]{4,0,3,1,2:T(8,128)(2,1)S(1)}, bf16[16,64,1,8,72]{4,0,3,1,2:T(8,128)(2,1)}, u32[]{:S(2)}) copy-start(bf16[16,64,1,8,72]{4,0,3,1,2:T(8,128)(2,1)} %copy.23) | copy-start | bytes 3538948
